TPU v7x, 32 devices: a whole 2x2x4 slice. The times are simulated.
32 devices in a mesh: replica: 4 (over y, core), shard: 8 (over z, x).
Axes of the slice: x: 2, y: 2, z: 4, core: 2. Of those that a mesh axis runs over, the one named last changes fastest.
Arguments:
- anchor: float32 [384, 8192], P('shard'), may hold values from -6 to 6
- replica_rows: bfloat16 [4, 384, 8192], P('replica', 'shard'), may hold values from -6 to 6
- outer_velocity: float32 [384, 8192], P('shard', 'replica'), may hold values from -6 to 6
- features: bfloat16 [4, 384, 256], P('replica', 'shard'), may hold values from -6 to 6
- cotangent: bfloat16 [4, 256, 1024], P('replica', 'shard'), may hold values from -0.375 to 0.375
- inner_weight: float32 [4, 384, 1024], P('replica', 'shard'), may hold values from -6 to 6
- first_moment: float32 [4, 384, 1024], P('replica', 'shard'), may hold values from -6 to 6
- second_moment: float32 [4, 384, 1024], P('replica', 'shard'), may hold values from 0.5 to 2
Outputs:
- new_anchor: float32 [384, 8192], P('shard')
- merged_rows: bfloat16 [4, 384, 8192], P('replica', 'shard')
- new_velocity: float32 [384, 8192], P('shard', 'replica')
- new_weight: float32 [4, 384, 1024], P('replica', 'shard')
- new_first: float32 [4, 384, 1024], P('replica', 'shard')
- new_second: float32 [4, 384, 1024], P('replica', 'shard')
All inputs are finite; a program needn't handle non-finite values.
Results may differ from a plain program's by a relative error of at most 0.0035.
Values may be sent and summed in bfloat16 or wider, within the bound.
A program may use at most 64 MiB of HBM per device.

v0:
```python
import jax
import jax.numpy as jnp
from jax import lax
from jax.sharding import PartitionSpec as P

momentum_keep = 0.9
outer_rate = 0.7
blend_keep = 0.5
inner_rate = 0.01
decay_first = 0.9
decay_second = 0.95
weight_decay = 0.1
epsilon = 1e-08
first_fix = 1.0 - 0.9**10
second_fix = 1.0 - 0.95**10


def outer_sync(anchor, replica_rows, outer_velocity):
    replicas = lax.axis_size("replica")
    own_rows = replica_rows[0].astype(jnp.float32)
    slice_width = outer_velocity.shape[1]
    offset = lax.axis_index("replica") * slice_width
    drift = anchor - own_rows
    summed = lax.psum(drift, "replica")
    velocity_all = lax.all_gather(
        outer_velocity.astype(jnp.bfloat16), "replica", axis=1, tiled=True
    ).astype(outer_velocity.dtype)
    outer_grad = summed / replicas
    velocity_next = momentum_keep * velocity_all + outer_grad
    new_anchor = anchor - outer_rate * (outer_grad + momentum_keep * velocity_next)
    new_velocity = lax.dynamic_slice_in_dim(velocity_next, offset, slice_width, 1)
    merged_rows = (blend_keep * own_rows + (1.0 - blend_keep) * new_anchor).astype(jnp.bfloat16)
    return (new_anchor, merged_rows[None], new_velocity)


def inner_update(features, cotangent, inner_weight, first_moment, second_moment):
    feature_rows = features[0]
    gradient = jnp.dot(
        feature_rows,
        lax.all_gather(cotangent, "shard", axis=1, tiled=True)[0],
        preferred_element_type=jnp.float32,
    )[None]
    new_first = decay_first * first_moment + (1.0 - decay_first) * gradient
    new_second = decay_second * second_moment + (1.0 - decay_second) * gradient * gradient
    stepped = new_first / first_fix / (jnp.sqrt(new_second / second_fix) + epsilon)
    new_weight = inner_weight - inner_rate * (stepped + weight_decay * inner_weight)
    return (new_weight, new_first, new_second)


def local(
    anchor,
    replica_rows,
    outer_velocity,
    features,
    cotangent,
    inner_weight,
    first_moment,
    second_moment,
):
    new_weight, new_first, new_second = inner_update(
        features, cotangent, inner_weight, first_moment, second_moment
    )
    new_anchor, merged_rows, new_velocity = outer_sync(anchor, replica_rows, outer_velocity)
    return (new_anchor, merged_rows, new_velocity, new_weight, new_first, new_second)


def solution(mesh):
    in_specs = (
        P("shard", None),
        P("replica", "shard", None),
        P("shard", "replica"),
        P("replica", "shard", None),
        P("replica", "shard", None),
        P("replica", "shard", None),
        P("replica", "shard", None),
        P("replica", "shard", None),
    )
    out_specs = (
        P("shard", None),
        P("replica", "shard", None),
        P("shard", "replica"),
        P("replica", "shard", None),
        P("replica", "shard", None),
        P("replica", "shard", None),
    )
    return jax.shard_map(local, mesh=mesh, in_specs=in_specs, out_specs=out_specs, check_vma=False)
```

profile of v0, /device:TPU:0, one launch (start us, length us, event | category | flops | bytes accessed | tf_op | source)
XLA Modules:
  0.0 71.8 jit_solution(1049866319276950009)
XLA Ops:
  7.2 0.0 copy-start
  7.2 0.0 all-reduce.2.cloned.1.call-start
  7.2 2.9 %convert_subtract_fusion = f32[48,8192]{1,0:T(8,128)} fusion(f32[48,8192]{1,0:T(8,128)} %param.8, bf16[1,48,8192]{2,1,0:T(8,128)(2,1)} %param.9), kind=kLoop, calls=%fused_computation.1 | loop fusion | flops 786432 | bytes 3932160 | tf_op jit(solution)/shard_map/sub | solution.py:23
  10.1 0.0 copy-start.3
  10.1 0.0 copy-start.7
  10.1 0.0 copy-start.4
  10.1 0.0 copy-start.5
  10.1 0.0 copy-start.6
  10.1 0.0 all-reduce.2.cloned.1.call-update
  10.2 0.9 %copy-done.3 = f32[48,2048]{1,0:T(8,128)S(1)} copy-done((f32[48,2048]{1,0:T(8,128)S(1)}, f32[48,2048]{1,0:T(8,128)}, u32[]{:S(2)}) %copy-start.3) | copy-done | bytes 393240
  11.1 0.0 copy-done.7
  11.1 0.0 copy-start.1
  11.2 0.0 copy-start.2
  11.2 33.3 %all_gather.7 = bf16[1,256,1024]{2,1,0:T(8,128)(2,1)S(1)} all-gather(bf16[1,32,1024]{2,1,0:T(8,128)(2,1)S(1)} %copy-done.7), channel_id=1, replica_groups=mesh['replica'=4,'shard'=8] {'shard'}, dimensions={1}, use_global_device_ids=true | all-gather | bytes 589824 | tf_op jit(solution)/shard_map/all_gather | solution.py:40
  44.4 0.0 copy-done
  44.4 0.0 copy-done.4
  44.4 0.0 copy-done.5
  44.5 0.0 copy-done.6
  44.5 1.1 %multiply_subtract_fusion.1 = (f32[1,48,1024]{2,1,0:T(8,128)}, f32[1,48,1024]{2,1,0:T(8,128)}, f32[1,48,1024]{2,1,0:T(8,128)}) fusion(f32[1,48,1024]{2,1,0:T(8,128)S(1)} %copy-done.4, f32[1,48,1024]{2,1,0:T(8,128)S(1)} %copy-done.5, f32[1,48,1024]{2,1,0:T(8,128)S(1)} %copy-done.6, bf16[1,256,1024]{2,1,0:T(8,128)(2,1)S(1)} %all_gather.7, ...), kind=kOutput, calls=%fused_computation.13 | convolution fusion | flops 25903104 | bytes 1728512 | tf_op jit(solution)/shard_map/dot_general | solution.py:38
  45.6 13.3 %all_gather.6 = bf16[48,8192]{1,0:T(8,128)(2,1)S(1)} all-gather(bf16[48,2048]{1,0:T(8,128)(2,1)S(1)} %convert_element_type.17), channel_id=1, replica_groups=mesh['replica'=4,'shard'=8] {'replica'}, dimensions={1}, use_global_device_ids=true | all-gather | bytes 983040 | tf_op jit(solution)/shard_map/all_gather | solution.py:25
  58.9 1.9 %all-reduce.2.cloned.1.call-done = f32[48,8192]{1,0:T(8,128)} async-done(((f32[48,8192]{1,0:T(8,128)}), f32[48,8192]{1,0:T(8,128)}) %all-reduce.2.cloned.1.call-update) | async-done | bytes 1572880 | tf_op jit(solution)/shard_map/psum | solution.py:24
  60.8 0.0 copy-done.1
  60.8 0.0 copy-done.2
  60.8 3.4 %fusion.2 = (bf16[1,48,8192]{2,1,0:T(8,128)(2,1)}, f32[48,8192]{1,0:T(8,128)}, f32[48,8192]{1,0:T(8,128)S(1)}) fusion(bf16[1,48,8192]{2,1,0:T(8,128)(2,1)S(1)} %copy-done.2, f32[48,8192]{1,0:T(8,128)S(1)} %copy-done.1, bf16[48,8192]{1,0:T(8,128)(2,1)S(1)} %all_gather.6, f32[48,8192]{1,0:T(8,128)} %all-reduce.2.cloned.1.call-done), kind=kLoop, calls=%fused_computation.6 | loop fusion | flops 4718592 | bytes 8650752 | tf_op jit(solution)/shard_map/broadcast_in_dim | solution.py:33
  64.2 0.8 %constant_dynamic-slice_fusion = f32[48,2048]{1,0:T(8,128)} fusion(f32[48,8192]{1,0:T(8,128)S(1)} %get-tuple-element.11, s32[]{:T(128)S(6)} %select_n.3), kind=kLoop, calls=%fused_computation.15 | loop fusion | bytes 786436 | tf_op jit(solution)/shard_map/dynamic_slice | solution.py:31
  (1 shorter events, 0.0 us)
Async XLA Ops:
  7.2 37.3 %copy-start = (bf16[1,48,256]{2,1,0:T(8,128)(2,1)S(1)}, bf16[1,48,256]{2,1,0:T(8,128)(2,1)}, u32[]{:S(2)}) copy-start(bf16[1,48,256]{2,1,0:T(8,128)(2,1)} %param.11) | copy-start | bytes 73732
  7.2 53.6 %all-reduce.2.cloned.1.call-start = ((), (), s32[]{:S(2)}) async-start(), calls=%async_computation | async-start | bytes 3145728 | tf_op jit(solution)/shard_map/psum | solution.py:24
  10.1 1.0 %copy-start.3 = (f32[48,2048]{1,0:T(8,128)S(1)}, f32[48,2048]{1,0:T(8,128)}, u32[]{:S(2)}) copy-start(f32[48,2048]{1,0:T(8,128)} %param.10) | copy-start | bytes 1179652
  10.1 1.0 %copy-start.7 = (bf16[1,32,1024]{2,1,0:T(8,128)(2,1)S(1)}, bf16[1,32,1024]{2,1,0:T(8,128)(2,1)}, u32[]{:S(2)}) copy-start(bf16[1,32,1024]{2,1,0:T(8,128)(2,1)} %param.12) | copy-start | bytes 196612
  10.1 34.3 %copy-start.4 = (f32[1,48,1024]{2,1,0:T(8,128)S(1)}, f32[1,48,1024]{2,1,0:T(8,128)}, u32[]{:S(2)}) copy-start(f32[1,48,1024]{2,1,0:T(8,128)} %param.13) | copy-start | bytes 589828
  10.1 34.3 %copy-start.5 = (f32[1,48,1024]{2,1,0:T(8,128)S(1)}, f32[1,48,1024]{2,1,0:T(8,128)}, u32[]{:S(2)}) copy-start(f32[1,48,1024]{2,1,0:T(8,128)} %param.14) | copy-start | bytes 589828
  10.1 34.3 %copy-start.6 = (f32[1,48,1024]{2,1,0:T(8,128)S(1)}, f32[1,48,1024]{2,1,0:T(8,128)}, u32[]{:S(2)}) copy-start(f32[1,48,1024]{2,1,0:T(8,128)} %param.15) | copy-start | bytes 589828
  11.1 49.6 %copy-start.1 = (f32[48,8192]{1,0:T(8,128)S(1)}, f32[48,8192]{1,0:T(8,128)}, u32[]{:S(2)}) copy-start(f32[48,8192]{1,0:T(8,128)} %param.8) | copy-start | bytes 4718596
  11.2 49.6 %copy-start.2 = (bf16[1,48,8192]{2,1,0:T(8,128)(2,1)S(1)}, bf16[1,48,8192]{2,1,0:T(8,128)(2,1)}, u32[]{:S(2)}) copy-start(bf16[1,48,8192]{2,1,0:T(8,128)(2,1)} %param.9) | copy-start | bytes 2359300
Sparse Core Ops, SparseCore 0:
  10.9 49.7 all-reduce.1
where the time goes:
time: 72 us; the launch traced here: 71.8 us
  blocking collectives  46.6 us (65%)
  between operations  14.1 us (20%)
  other arithmetic  6.34 us (9%)
  waiting for transfers between devices  1.87 us (3%)
  local copies, waits for them, and re-layouts  1.75 us (2%)
  matrix products  1.11 us (2%)
    all_gather x1, blocking collectives, inner_update(): lax.all_gather(cotangent, 'shard', axis=1, tiled=True)[0]  33.3 us
    all_gather x1, blocking collectives, outer_sync(): lax.all_gather(outer_velocity.astype(jnp.bfloat16), 'replica', axis=1, ti...  13.3 us
    broadcast_in_dim x1, other arithmetic, outer_sync(): return (new_anchor, merged_rows[None], new_velocity)  3.43 us
    sub x1, other arithmetic, outer_sync(): drift = anchor - own_rows  2.88 us
    psum x1, waiting for transfers between devices, outer_sync(): summed = lax.psum(drift, 'replica')  1.86 us
  transfers between devices with their start and end apart: 1, of which 1 were waited for; matrix products, arithmetic and copies ran while one was open for 2% of the time, Pallas kernels for 0%

commit v1 on v0

v1 whole, which is shorter than its diff:
```python
import functools

import jax
import jax.numpy as jnp
from jax import lax
from jax.experimental import pallas as pl
from jax.experimental.pallas import tpu as pltpu
from jax.sharding import PartitionSpec as P

momentum_keep = 0.9
outer_rate = 0.7
blend_keep = 0.5
inner_rate = 0.01
decay_first = 0.9
decay_second = 0.95
weight_decay = 0.1
epsilon = 1e-08
first_fix = 1.0 - 0.9**10
second_fix = 1.0 - 0.95**10

MESH = pl.DeviceIdType.MESH
SPLIT = 4


def kernel(R, S, anchor_h, rows_h, vel_h, feat_h, cot_h, w_h, m_h, s_h,
           na_o, mg_o, nv_o, nw_o, nm_o, ns_o,
           anchor, rows, vel, feat, cot, w, m, s, sib_rows, msg,
           in_sem, sib_send, sib_recv, y_send, fwd_send, msg_recv,
           cot_own_send, cot_z_send, cot_x_send, cot_recv):
    C = R // 2
    H = SPLIT
    me, at = lax.axis_index("replica"), lax.axis_index("shard")
    y, c = me // 2, me % 2
    sib = me + 1 - 2 * c
    partner = at + 1 - 2 * (at % 2)
    pos, length = at // 2, S // 2
    W = vel.shape[1]
    piece = W // H
    depth = cot_h.shape[1]

    def columns(q, h):
        return pl.ds(pl.multiple_of(q * W + h * piece, 128), piece)

    def quarter(q):
        return pl.ds(pl.multiple_of(q * W, 128), W)

    def tokens(k):
        return pl.ds(pl.multiple_of(k * depth, depth), depth)

    barrier = pltpu.get_barrier_semaphore()
    pl.semaphore_signal(barrier, inc=1, device_id={"replica": sib}, device_id_type=MESH)
    for t in range(1, C):
        pl.semaphore_signal(barrier, inc=1, device_id={"replica": lax.rem(me + 2 * t, R)}, device_id_type=MESH)
    pl.semaphore_signal(barrier, inc=1, device_id={"shard": partner}, device_id_type=MESH)

    @pl.when(pos > 0)
    def _():
        pl.semaphore_signal(barrier, inc=1, device_id={"shard": at - 2}, device_id_type=MESH)

    @pl.when(pos < length - 1)
    def _():
        pl.semaphore_signal(barrier, inc=1, device_id={"shard": at + 2}, device_id_type=MESH)

    loads = {}
    slot = 0

    def load(name, src, dst):
        nonlocal slot
        copy = pltpu.make_async_copy(src, dst, in_sem.at[slot])
        copy.start()
        slot += 1
        loads[name] = copy

    load("cot", cot_h.at[0], cot.at[tokens(at)])
    for j in range(C):
        q = 2 * j + 1 - c
        load(("out", j), rows_h.at[0, :, quarter(q)], rows.at[:, quarter(q)])
    for j in range(C):
        q = 2 * j + c
        load(("keep", j), rows_h.at[0, :, quarter(q)], rows.at[:, quarter(q)])
    load("anchor", anchor_h, anchor)
    load("vel", vel_h, vel)
    load("feat", feat_h.at[0], feat)
    load("w", w_h.at[0], w)
    load("m", m_h.at[0], m)
    load("s", s_h.at[0], s)

    count = 2 + (C - 1) + (pos > 0).astype(jnp.int32) + (pos < length - 1).astype(jnp.int32)
    pl.semaphore_wait(barrier, count)

    def sib_copy(j, h):
        return pltpu.make_async_remote_copy(
            src_ref=rows.at[:, columns(2 * j + 1 - c, h)], dst_ref=sib_rows.at[j, h],
            send_sem=sib_send.at[j, h], recv_sem=sib_recv.at[j, h],
            device_id={"replica": sib}, device_id_type=MESH)

    def cot_copy(k, send_sem, target):
        return pltpu.make_async_remote_copy(
            src_ref=cot.at[tokens(k)], dst_ref=cot.at[tokens(k)],
            send_sem=send_sem, recv_sem=cot_recv.at[k],
            device_id={"shard": target}, device_id_type=MESH)

    for j in range(C):
        loads[("out", j)].wait()
        for h in range(H):
            sib_copy(j, h).start()

    loads["cot"].wait()
    cot_right = cot_copy(at, cot_own_send.at[0], at + 2)
    cot_left = cot_copy(at, cot_own_send.at[1], at - 2)
    cot_across = cot_copy(at, cot_own_send.at[2], partner)

    @pl.when(pos < length - 1)
    def _():
        cot_right.start()

    @pl.when(pos > 0)
    def _():
        cot_left.start()

    cot_across.start()

    def y_copy(t, j, h):
        return pltpu.make_async_remote_copy(
            src_ref=msg.at[c, y, j, h], dst_ref=msg.at[c, y, j, h],
            send_sem=y_send.at[t - 1, j, h], recv_sem=msg_recv.at[c, y, j, h],
            device_id={"replica": lax.rem(me + 2 * t, R)}, device_id_type=MESH)

    def to_sib(src, j, h):
        return pltpu.make_async_remote_copy(
            src_ref=msg.at[c, src, j, h], dst_ref=msg.at[c, src, j, h],
            send_sem=fwd_send.at[src, j, h], recv_sem=msg_recv.at[c, src, j, h],
            device_id={"replica": sib}, device_id_type=MESH)

    def arrival(p, src, j, h):
        return pltpu.make_async_remote_copy(
            src_ref=msg.at[p, src, j, h], dst_ref=msg.at[p, src, j, h],
            send_sem=fwd_send.at[src, j, h], recv_sem=msg_recv.at[p, src, j, h],
            device_id={"replica": sib}, device_id_type=MESH)

    c1 = outer_rate * (1.0 + momentum_keep)
    c2 = outer_rate * momentum_keep * momentum_keep
    share = c1 / R
    for j in range(C):
        loads[("keep", j)].wait()
        if j == 0:
            loads["anchor"].wait()
            loads["vel"].wait()
        mine = y == j
        of_anchor = jnp.where(mine, 0.0, 2.0)
        of_rows = jnp.where(mine, share, -1.0)
        of_vel = jnp.where(mine, -c2, 0.0)
        for h in range(H):
            sib_copy(j, h).wait_recv()
            cols = columns(2 * j + c, h)
            both = rows[:, cols].astype(jnp.float32) + sib_rows[j, h].astype(jnp.float32)
            value = of_anchor * anchor[:, cols] + of_rows * both
            value = value + of_vel * vel[:, h * piece:(h + 1) * piece]
            msg[c, y, j, h] = value.astype(jnp.bfloat16)
            for t in range(1, C):
                y_copy(t, j, h).start()
            to_sib(y, j, h).start()

    def finish(p, j, h):
        cols = columns(2 * j + p, h)
        others = msg[p, (j + 1) % C, j, h].astype(jnp.float32)
        for t in range(2, C):
            others = others + msg[p, (j + t) % C, j, h].astype(jnp.float32)
        own = msg[p, j, j, h].astype(jnp.float32)
        new_anchor = (1.0 - 2.0 * share) * anchor[:, cols] + own - share * others
        na_o[:, cols] = new_anchor
        mg_o[0, :, cols] = (
            blend_keep * rows[:, cols].astype(jnp.float32) + (1.0 - blend_keep) * new_anchor
        ).astype(jnp.bfloat16)

    def finish_velocity(j, h):
        @pl.when(y == j)
        def _():
            cols = columns(2 * j + c, h)
            part = slice(h * piece, (h + 1) * piece)
            total = 2.0 * anchor[:, cols] - (
                rows[:, cols].astype(jnp.float32) + sib_rows[j, h].astype(jnp.float32))
            for t in range(1, C):
                total = total + msg[c, (j + t) % C, j, h].astype(jnp.float32)
            nv_o[:, part] = momentum_keep * vel[:, part] + total / R

    def finish_sib(j, h):
        for src in range(C):
            arrival(1 - c, src, j, h).wait_recv()
        finish(1 - c, j, h)

    def cot_step(t):
        @pl.when(pos >= t)
        def _():
            k = at - 2 * t
            cot_copy(k, cot_x_send.at[0], partner).wait_recv()

            @pl.when(pos < length - 1)
            def _():
                cot_copy(k, cot_z_send.at[0, t - 1], at + 2).start()

            cot_copy(k, cot_x_send.at[k // 2], partner).start()

        @pl.when(pos + t < length)
        def _():
            k = at + 2 * t
            cot_copy(k, cot_x_send.at[0], partner).wait_recv()

            @pl.when(pos > 0)
            def _():
                cot_copy(k, cot_z_send.at[1, t - 1], at - 2).start()

            cot_copy(k, cot_x_send.at[k // 2], partner).start()

    steps = length - 1
    pieces = [(j, h) for j in range(C) for h in range(H)]
    done = 0
    before = None
    for i, (j, h) in enumerate(pieces):
        for t in range(1, C):
            src = lax.rem(y + t, C)
            arrival(c, src, j, h).wait_recv()
            to_sib(src, j, h).start()
        finish(c, j, h)
        finish_velocity(j, h)
        if before is not None:
            finish_sib(*before)
        before = (j, h)
        goal = min(steps, (i + 1) * steps // (len(pieces) - 1))
        while done < goal:
            done += 1
            cot_step(done)

    for k in range(length):
        cot_copy(2 * k + 1 - at % 2, cot_x_send.at[0], partner).wait_recv()
    for name in ("feat", "w", "m", "s"):
        loads[name].wait()
    tile = min(256, w.shape[1])
    for n in range(w.shape[1] // tile):
        part = slice(n * tile, (n + 1) * tile)
        gradient = jnp.dot(feat[...], cot[:, part], preferred_element_type=jnp.float32)
        new_first = decay_first * m[:, part] + (1.0 - decay_first) * gradient
        new_second = decay_second * s[:, part] + (1.0 - decay_second) * gradient * gradient
        stepped = new_first / first_fix / (jnp.sqrt(new_second / second_fix) + epsilon)
        weight = w[:, part]
        nw_o[0, :, part] = weight - inner_rate * (stepped + weight_decay * weight)
        nm_o[0, :, part] = new_first
        ns_o[0, :, part] = new_second

    finish_sib(*before)

    for j, h in pieces:
        sib_copy(j, h).wait_send()
        for t in range(1, C):
            y_copy(t, j, h).wait_send()
        for src in range(C):
            to_sib(src, j, h).wait_send()
    cot_across.wait_send()

    @pl.when(pos < length - 1)
    def _():
        cot_right.wait_send()

    @pl.when(pos > 0)
    def _():
        cot_left.wait_send()

    for t in range(1, length):
        @pl.when(pos >= t)
        def _():
            @pl.when(pos < length - 1)
            def _():
                cot_copy(at - 2 * t, cot_z_send.at[0, t - 1], at + 2).wait_send()

            cot_copy(at - 2 * t, cot_x_send.at[(at - 2 * t) // 2], partner).wait_send()

        @pl.when(pos + t < length)
        def _():
            @pl.when(pos > 0)
            def _():
                cot_copy(at + 2 * t, cot_z_send.at[1, t - 1], at - 2).wait_send()

            cot_copy(at + 2 * t, cot_x_send.at[(at + 2 * t) // 2], partner).wait_send()


def local(R, S, anchor, replica_rows, outer_velocity, features, cotangent,
          inner_weight, first_moment, second_moment):
    C, H = R // 2, SPLIT
    depth_rows = anchor.shape[0]
    W = outer_velocity.shape[1]
    f32, bf16 = jnp.float32, jnp.bfloat16
    args = (anchor, replica_rows, outer_velocity, features, cotangent,
            inner_weight, first_moment, second_moment)
    outs = (anchor, replica_rows, outer_velocity, inner_weight, first_moment, second_moment)
    dma = pltpu.SemaphoreType.DMA
    length = S // 2
    room = 67043328 - sum(a.size * a.dtype.itemsize for a in outs) - 2**16
    return pl.pallas_call(
        functools.partial(kernel, R, S),
        out_shape=tuple(pltpu.VMEM(a.shape, a.dtype) for a in outs),
        in_specs=[pl.BlockSpec(memory_space=pltpu.HBM)] * len(args),
        out_specs=tuple(pl.BlockSpec(memory_space=pltpu.VMEM) for _ in outs),
        scratch_shapes=[
            pltpu.VMEM(anchor.shape, f32),
            pltpu.VMEM(replica_rows.shape[1:], bf16),
            pltpu.VMEM(outer_velocity.shape, f32),
            pltpu.VMEM(features.shape[1:], bf16),
            pltpu.VMEM((S * cotangent.shape[1], cotangent.shape[2]), bf16),
            pltpu.VMEM(inner_weight.shape[1:], f32),
            pltpu.VMEM(inner_weight.shape[1:], f32),
            pltpu.VMEM(inner_weight.shape[1:], f32),
            pltpu.VMEM((C, H, depth_rows, W // H), bf16),
            pltpu.VMEM((2, C, C, H, depth_rows, W // H), bf16),
            dma((7 + 2 * C,)),
            dma((C, H)),
            dma((C, H)),
            dma((C - 1, C, H)),
            dma((C, C, H)),
            dma((2, C, C, H)),
            dma((3,)),
            dma((2, max(length - 1, 1))),
            dma((length,)),
            dma((S,)),
        ],
        compiler_params=pltpu.CompilerParams(
            collective_id=0, has_side_effects=True, vmem_limit_bytes=room),
    )(*args)


def solution(mesh):
    in_specs = (
        P("shard", None),
        P("replica", "shard", None),
        P("shard", "replica"),
        P("replica", "shard", None),
        P("replica", "shard", None),
        P("replica", "shard", None),
        P("replica", "shard", None),
        P("replica", "shard", None),
    )
    out_specs = (
        P("shard", None),
        P("replica", "shard", None),
        P("shard", "replica"),
        P("replica", "shard", None),
        P("replica", "shard", None),
        P("replica", "shard", None),
    )
    body = functools.partial(local, mesh.shape["replica"], mesh.shape["shard"])
    return jax.shard_map(body, mesh=mesh, in_specs=in_specs, out_specs=out_specs, check_vma=False)
```

time: 72 us -> 28.5 us (0.40)
  blocking collectives: 46.6 us -> 0 us
  Pallas kernels: 0 us -> 22.9 us
  between operations: 14.1 us -> 0.65 us
  other arithmetic: 6.34 us -> 0 us
  local copies, waits for them, and re-layouts: 1.75 us -> 4.8 us
  waiting for transfers between devices: 1.87 us -> 0 us
  matrix products: 1.11 us -> 0 us
    all_gather x2 -> x0, blocking collectives: 46.6 us -> none  [the longest x1 33.3 us: inner_update(): lax.all_gather(cotangent, 'shard', axis=1, tiled=True)[0]]
    pallas_call x0 -> x1, Pallas kernels: none -> 22.9 us  [local(): pl.pallas_call(functools.partial(kernel, R, S), out_shape=tuple((pltpu.VM...]
    unnamed x16 -> x6, local copies, waits for them, and re-layouts: 0.98 us -> 4.8 us
    broadcast_in_dim x1 -> x0, other arithmetic: 3.43 us -> none  [outer_sync(): return (new_anchor, merged_rows[None], new_velocity)]
    sub x1 -> x0, other arithmetic: 2.88 us -> none  [outer_sync(): drift = anchor - own_rows]
    psum x1 -> x0, waiting for transfers between devices: 1.86 us -> none  [outer_sync(): summed = lax.psum(drift, 'replica')]
    dot_general x1 -> x0, matrix products: 1.11 us -> none  [inner_update(): jnp.dot(feature_rows, lax.all_gather(cotangent, 'shard', axis=1, tiled=Tr...]
    dynamic_slice x1 -> x0, local copies, waits for them, and re-layouts: 0.77 us -> none  [outer_sync(): lax.dynamic_slice_in_dim(velocity_next, offset, slice_width, 1)]
  transfers between devices with their start and end apart: 1 -> 0, of which waited for: 1 -> 0; matrix products, arithmetic and copies ran while one was open for 2% -> 0% of each run, Pallas kernels for 0% -> 0%
where the time goes in v1:
time: 28.5 us; the launch traced here: 28.4 us
  Pallas kernels  22.9 us (80%)
  local copies, waits for them, and re-layouts  4.8 us (17%)
  between operations  0.65 us (2%)
    pallas_call x1, Pallas kernels, local(): pl.pallas_call(functools.partial(kernel, R, S), out_shape=tuple((pltpu.VM...  22.9 us
    unnamed x6, local copies, waits for them, and re-layouts  4.8 us

profile of v1, /device:TPU:0, one launch (start us, length us, event | category | flops | bytes accessed | tf_op | source)
XLA Modules:
  0.0 28.4 jit_solution(16560207258861618801)
XLA Ops:
  0.6 22.9 %shard_map.127 = (f32[48,8192]{1,0:T(8,128)S(1)}, bf16[1,48,8192]{2,1,0:T(8,128)(2,1)S(1)}, f32[48,2048]{1,0:T(8,128)S(1)}, f32[1,48,1024]{2,1,0:T(8,128)S(1)}, ...) custom-call(f32[48,8192]{1,0:T(8,128)} %anchor_h.1, bf16[1,48,8192]{2,1,0:T(8,128)(2,1)} %rows_h.1, ...), custom_call_target="tpu_custom_call" | custom-call | tf_op jit(solution)/shard_map/pallas_call | solution.py:298
  23.6 1.1 %copy.20 = f32[48,8192]{1,0:T(8,128)} copy(f32[48,8192]{1,0:T(8,128)S(1)} %get-tuple-element.6) | data formatting | bytes 3145728
  24.7 0.7 %copy.23 = f32[1,48,1024]{2,1,0:T(8,128)} copy(f32[1,48,1024]{2,1,0:T(8,128)S(1)} %get-tuple-element.9) | data formatting | bytes 393216
  25.4 0.7 %copy.24 = f32[1,48,1024]{2,1,0:T(8,128)} copy(f32[1,48,1024]{2,1,0:T(8,128)S(1)} %get-tuple-element.10) | data formatting | bytes 393216
  26.1 0.7 %copy.25 = f32[1,48,1024]{2,1,0:T(8,128)} copy(f32[1,48,1024]{2,1,0:T(8,128)S(1)} %get-tuple-element.11) | data formatting | bytes 393216
  26.7 0.7 %copy.22 = f32[48,2048]{1,0:T(8,128)} copy(f32[48,2048]{1,0:T(8,128)S(1)} %get-tuple-element.8) | data formatting | bytes 786432
  27.5 0.9 %copy.21 = bf16[1,48,8192]{2,1,0:T(8,128)(2,1)} copy(bf16[1,48,8192]{2,1,0:T(8,128)(2,1)S(1)} %get-tuple-element.7) | data formatting | bytes 1572864

commit v2 on v1

--- a/solution.py
+++ b/solution.py
@@ -20,6 +20,7 @@
 
 MESH = pl.DeviceIdType.MESH
 SPLIT = 4
+PARTS = 2
 
 
 def kernel(R, S, anchor_h, rows_h, vel_h, feat_h, cot_h, w_h, m_h, s_h,
@@ -37,6 +38,7 @@
     W = vel.shape[1]
     piece = W // H
     depth = cot_h.shape[1]
+    part_depth = depth // PARTS
 
     def columns(q, h):
         return pl.ds(pl.multiple_of(q * W + h * piece, 128), piece)
@@ -46,6 +48,9 @@
 
     def tokens(k):
         return pl.ds(pl.multiple_of(k * depth, depth), depth)
+
+    def half_tokens(k, u):
+        return pl.ds(pl.multiple_of(k * depth + u * part_depth, part_depth), part_depth)
 
     barrier = pltpu.get_barrier_semaphore()
     pl.semaphore_signal(barrier, inc=1, device_id={"replica": sib}, device_id_type=MESH)
@@ -94,10 +99,10 @@
             send_sem=sib_send.at[j, h], recv_sem=sib_recv.at[j, h],
             device_id={"replica": sib}, device_id_type=MESH)
 
-    def cot_copy(k, send_sem, target):
-        return pltpu.make_async_remote_copy(
-            src_ref=cot.at[tokens(k)], dst_ref=cot.at[tokens(k)],
-            send_sem=send_sem, recv_sem=cot_recv.at[k],
+    def cot_copy(k, u, send_sem, target):
+        return pltpu.make_async_remote_copy(
+            src_ref=cot.at[half_tokens(k, u)], dst_ref=cot.at[half_tokens(k, u)],
+            send_sem=send_sem.at[u], recv_sem=cot_recv.at[k, u],
             device_id={"shard": target}, device_id_type=MESH)
 
     for j in range(C):
@@ -106,19 +111,22 @@
             sib_copy(j, h).start()
 
     loads["cot"].wait()
-    cot_right = cot_copy(at, cot_own_send.at[0], at + 2)
-    cot_left = cot_copy(at, cot_own_send.at[1], at - 2)
-    cot_across = cot_copy(at, cot_own_send.at[2], partner)
+    cot_right = [cot_copy(at, u, cot_own_send.at[0], at + 2) for u in range(PARTS)]
+    cot_left = [cot_copy(at, u, cot_own_send.at[1], at - 2) for u in range(PARTS)]
+    cot_across = [cot_copy(at, u, cot_own_send.at[2], partner) for u in range(PARTS)]
 
     @pl.when(pos < length - 1)
     def _():
-        cot_right.start()
+        for copy in cot_right:
+            copy.start()
 
     @pl.when(pos > 0)
     def _():
-        cot_left.start()
-
-    cot_across.start()
+        for copy in cot_left:
+            copy.start()
+
+    for copy in cot_across:
+        copy.start()
 
     def y_copy(t, j, h):
         return pltpu.make_async_remote_copy(
@@ -189,34 +197,35 @@
             arrival(1 - c, src, j, h).wait_recv()
         finish(1 - c, j, h)
 
-    def cot_step(t):
+    def cot_step(t, u):
         @pl.when(pos >= t)
         def _():
             k = at - 2 * t
-            cot_copy(k, cot_x_send.at[0], partner).wait_recv()
+            cot_copy(k, u, cot_x_send.at[0], partner).wait_recv()
 
             @pl.when(pos < length - 1)
             def _():
-                cot_copy(k, cot_z_send.at[0, t - 1], at + 2).start()
-
-            cot_copy(k, cot_x_send.at[k // 2], partner).start()
+                cot_copy(k, u, cot_z_send.at[0, t - 1], at + 2).start()
+
+            cot_copy(k, u, cot_x_send.at[k // 2], partner).start()
 
         @pl.when(pos + t < length)
         def _():
             k = at + 2 * t
-            cot_copy(k, cot_x_send.at[0], partner).wait_recv()
+            cot_copy(k, u, cot_x_send.at[0], partner).wait_recv()
 
             @pl.when(pos > 0)
             def _():
-                cot_copy(k, cot_z_send.at[1, t - 1], at - 2).start()
-
-            cot_copy(k, cot_x_send.at[k // 2], partner).start()
-
-    steps = length - 1
+                cot_copy(k, u, cot_z_send.at[1, t - 1], at - 2).start()
+
+            cot_copy(k, u, cot_x_send.at[k // 2], partner).start()
+
     pieces = [(j, h) for j in range(C) for h in range(H)]
-    done = 0
+    todo = [(t, u) for t in range(1, length) for u in range(PARTS)]
     before = None
     for i, (j, h) in enumerate(pieces):
+        while todo and 3 * (todo[0][0] - 1) + todo[0][1] <= i + 2:
+            cot_step(*todo.pop(0))
         for t in range(1, C):
             src = lax.rem(y + t, C)
             arrival(c, src, j, h).wait_recv()
@@ -226,13 +235,12 @@
         if before is not None:
             finish_sib(*before)
         before = (j, h)
-        goal = min(steps, (i + 1) * steps // (len(pieces) - 1))
-        while done < goal:
-            done += 1
-            cot_step(done)
+    for step in todo:
+        cot_step(*step)
 
     for k in range(length):
-        cot_copy(2 * k + 1 - at % 2, cot_x_send.at[0], partner).wait_recv()
+        for u in range(PARTS):
+            cot_copy(2 * k + 1 - at % 2, u, cot_x_send.at[0], partner).wait_recv()
     for name in ("feat", "w", "m", "s"):
         loads[name].wait()
     tile = min(256, w.shape[1])
@@ -255,32 +263,68 @@
             y_copy(t, j, h).wait_send()
         for src in range(C):
             to_sib(src, j, h).wait_send()
-    cot_across.wait_send()
+    for copy in cot_across:
+        copy.wait_send()
 
     @pl.when(pos < length - 1)
     def _():
-        cot_right.wait_send()
+        for copy in cot_right:
+            copy.wait_send()
 
     @pl.when(pos > 0)
     def _():
-        cot_left.wait_send()
-
-    for t in range(1, length):
+        for copy in cot_left:
+            copy.wait_send()
+
+    for t, u in [(t, u) for t in range(1, length) for u in range(PARTS)]:
         @pl.when(pos >= t)
         def _():
+            k = at - 2 * t
+
             @pl.when(pos < length - 1)
             def _():
-                cot_copy(at - 2 * t, cot_z_send.at[0, t - 1], at + 2).wait_send()
-
-            cot_copy(at - 2 * t, cot_x_send.at[(at - 2 * t) // 2], partner).wait_send()
+                cot_copy(k, u, cot_z_send.at[0, t - 1], at + 2).wait_send()
+
+            cot_copy(k, u, cot_x_send.at[k // 2], partner).wait_send()
 
         @pl.when(pos + t < length)
         def _():
+            k = at + 2 * t
+
             @pl.when(pos > 0)
             def _():
-                cot_copy(at + 2 * t, cot_z_send.at[1, t - 1], at - 2).wait_send()
-
-            cot_copy(at + 2 * t, cot_x_send.at[(at + 2 * t) // 2], partner).wait_send()
+                cot_copy(k, u, cot_z_send.at[1, t - 1], at - 2).wait_send()
+
+            cot_copy(k, u, cot_x_send.at[k // 2], partner).wait_send()
+
+
+def store_kernel(*refs):
+    sems = refs[-1]
+    count = (len(refs) - 1) // 2
+    copies = []
+    for source, target in zip(refs[:count], refs[count:-1]):
+        rows = source.shape[-2]
+        cuts = 3 if rows % 48 == 0 else 1
+        for n in range(cuts):
+            part = pl.ds(n * (rows // cuts), rows // cuts)
+            index = (0, part) if len(source.shape) == 3 else (part,)
+            copies.append(pltpu.make_async_copy(
+                source.at[index], target.at[index], sems.at[len(copies)]))
+    for copy in copies:
+        copy.start()
+    for copy in copies:
+        copy.wait()
+
+
+def store(*arrays):
+    return pl.pallas_call(
+        store_kernel,
+        out_shape=tuple(jax.ShapeDtypeStruct(a.shape, a.dtype) for a in arrays),
+        in_specs=[pl.BlockSpec(memory_space=pltpu.VMEM)] * len(arrays),
+        out_specs=tuple(pl.BlockSpec(memory_space=pltpu.HBM) for _ in arrays),
+        scratch_shapes=[pltpu.SemaphoreType.DMA((3 * len(arrays),))],
+        compiler_params=pltpu.CompilerParams(vmem_limit_bytes=2**20),
+    )(*arrays)
 
 
 def local(R, S, anchor, replica_rows, outer_velocity, features, cotangent,
@@ -295,7 +339,7 @@
     dma = pltpu.SemaphoreType.DMA
     length = S // 2
     room = 67043328 - sum(a.size * a.dtype.itemsize for a in outs) - 2**16
-    return pl.pallas_call(
+    results = pl.pallas_call(
         functools.partial(kernel, R, S),
         out_shape=tuple(pltpu.VMEM(a.shape, a.dtype) for a in outs),
         in_specs=[pl.BlockSpec(memory_space=pltpu.HBM)] * len(args),
@@ -317,14 +361,15 @@
             dma((C - 1, C, H)),
             dma((C, C, H)),
             dma((2, C, C, H)),
-            dma((3,)),
-            dma((2, max(length - 1, 1))),
-            dma((length,)),
-            dma((S,)),
+            dma((3, PARTS)),
+            dma((2, max(length - 1, 1), PARTS)),
+            dma((length, PARTS)),
+            dma((S, PARTS)),
         ],
         compiler_params=pltpu.CompilerParams(
             collective_id=0, has_side_effects=True, vmem_limit_bytes=room),
     )(*args)
+    return store(*results)
 
 
 def solution(mesh):

time: 28.5 us -> 21.4 us (0.75)
  local copies, waits for them, and re-layouts: 4.8 us -> 0 us
  Pallas kernels: 22.9 us -> 20.6 us
    unnamed x6 -> x0, local copies, waits for them, and re-layouts: 4.8 us -> none
    pallas_call x1, Pallas kernels: 22.9 us -> 18.8 us  [local(): pl.pallas_call(functools.partial(kernel, R, S), out_shape=tuple((pltpu.VM...]
    pallas_call x0 -> x1, Pallas kernels: none -> 1.87 us  [store(): pl.pallas_call(store_kernel, out_shape=tuple((jax.ShapeDtypeStruct(a.shap...]
where the time goes in v2:
time: 21.4 us; the launch traced here: 21.3 us
  Pallas kernels  20.6 us (96%)
  between operations  0.64 us (3%)
    pallas_call x1, Pallas kernels, local(): pl.pallas_call(functools.partial(kernel, R, S), out_shape=tuple((pltpu.VM...  18.8 us
    pallas_call x1, Pallas kernels, store(): pl.pallas_call(store_kernel, out_shape=tuple((jax.ShapeDtypeStruct(a.shap...  1.87 us

profile of v2, /device:TPU:0, one launch (start us, length us, event | category | flops | bytes accessed | tf_op | source)
XLA Modules:
  0.0 21.3 jit_solution(654472325496200330)
XLA Ops:
  0.6 18.8 %shard_map.127 = (f32[48,8192]{1,0:T(8,128)S(1)}, bf16[1,48,8192]{2,1,0:T(8,128)(2,1)S(1)}, f32[48,2048]{1,0:T(8,128)S(1)}, f32[1,48,1024]{2,1,0:T(8,128)S(1)}, ...) custom-call(f32[48,8192]{1,0:T(8,128)} %anchor_h.1, bf16[1,48,8192]{2,1,0:T(8,128)(2,1)} %rows_h.1, ...), custom_call_target="tpu_custom_call" | custom-call | tf_op jit(solution)/shard_map/pallas_call | solution.py:342
  19.4 1.9 %shard_map.128 = (f32[48,8192]{1,0:T(8,128)}, bf16[1,48,8192]{2,1,0:T(8,128)(2,1)}, f32[48,2048]{1,0:T(8,128)}, f32[1,48,1024]{2,1,0:T(8,128)}, f32[1,48,1024]{2,1,0:T(8,128)}, /*index=5*/f32[1,48,1024]{2,1,0:T(8,128)}) custom-call(f32[48,8192]{1,0:T(8,128)S(1)} %get-tuple-element.12.refs_0_, bf16[1,48,8192]{2,1,0:T(8,128)(2,1)S(1)} %get-tuple-element.13.refs_1_, ...), custom_call_target="tpu_custom_call" | custom-call | tf_op jit(solution)/shard_map/pallas_call | solution.py:320

commit v3 on v2

--- a/solution.py
+++ b/solution.py
@@ -23,25 +23,35 @@
 PARTS = 2
 
 
+def pieces_of(C, W):
+    even = W // SPLIT
+    pieces = [(j, h * even, even) for j in range(C) for h in range(SPLIT)]
+    if even > 128:
+        pieces = [(0, 0, 128), (0, 128, even - 128)] + pieces[1:]
+        j, offset, _ = pieces.pop()
+        pieces += [(j, offset, even - 128), (j, offset + even - 128, 128)]
+    return pieces
+
+
 def kernel(R, S, anchor_h, rows_h, vel_h, feat_h, cot_h, w_h, m_h, s_h,
            na_o, mg_o, nv_o, nw_o, nm_o, ns_o,
            anchor, rows, vel, feat, cot, w, m, s, sib_rows, msg,
-           in_sem, sib_send, sib_recv, y_send, fwd_send, msg_recv,
+           in_sem, sib_send, sib_recv, y_send, cross_send, fwd_send, msg_recv,
            cot_own_send, cot_z_send, cot_x_send, cot_recv):
     C = R // 2
-    H = SPLIT
     me, at = lax.axis_index("replica"), lax.axis_index("shard")
     y, c = me // 2, me % 2
     sib = me + 1 - 2 * c
     partner = at + 1 - 2 * (at % 2)
     pos, length = at // 2, S // 2
     W = vel.shape[1]
-    piece = W // H
+    pieces = pieces_of(C, W)
+    last = len(pieces) - 1
     depth = cot_h.shape[1]
     part_depth = depth // PARTS
 
-    def columns(q, h):
-        return pl.ds(pl.multiple_of(q * W + h * piece, 128), piece)
+    def columns(q, offset, width):
+        return pl.ds(pl.multiple_of(q * W + offset, 128), width)
 
     def quarter(q):
         return pl.ds(pl.multiple_of(q * W, 128), W)
@@ -56,6 +66,7 @@
     pl.semaphore_signal(barrier, inc=1, device_id={"replica": sib}, device_id_type=MESH)
     for t in range(1, C):
         pl.semaphore_signal(barrier, inc=1, device_id={"replica": lax.rem(me + 2 * t, R)}, device_id_type=MESH)
+        pl.semaphore_signal(barrier, inc=1, device_id={"replica": lax.rem(sib + 2 * t, R)}, device_id_type=MESH)
     pl.semaphore_signal(barrier, inc=1, device_id={"shard": partner}, device_id_type=MESH)
 
     @pl.when(pos > 0)
@@ -90,13 +101,15 @@
     load("m", m_h.at[0], m)
     load("s", s_h.at[0], s)
 
-    count = 2 + (C - 1) + (pos > 0).astype(jnp.int32) + (pos < length - 1).astype(jnp.int32)
+    count = 2 + 2 * (C - 1) + (pos > 0).astype(jnp.int32) + (pos < length - 1).astype(jnp.int32)
     pl.semaphore_wait(barrier, count)
 
-    def sib_copy(j, h):
+    def sib_copy(i):
+        j, offset, width = pieces[i]
         return pltpu.make_async_remote_copy(
-            src_ref=rows.at[:, columns(2 * j + 1 - c, h)], dst_ref=sib_rows.at[j, h],
-            send_sem=sib_send.at[j, h], recv_sem=sib_recv.at[j, h],
+            src_ref=rows.at[:, columns(2 * j + 1 - c, offset, width)],
+            dst_ref=sib_rows.at[j, :, pl.ds(offset, width)],
+            send_sem=sib_send.at[i], recv_sem=sib_recv.at[i],
             device_id={"replica": sib}, device_id_type=MESH)
 
     def cot_copy(k, u, send_sem, target):
@@ -105,10 +118,10 @@
             send_sem=send_sem.at[u], recv_sem=cot_recv.at[k, u],
             device_id={"shard": target}, device_id_type=MESH)
 
-    for j in range(C):
-        loads[("out", j)].wait()
-        for h in range(H):
-            sib_copy(j, h).start()
+    for i, (j, offset, width) in enumerate(pieces):
+        if offset == 0:
+            loads[("out", j)].wait()
+        sib_copy(i).start()
 
     loads["cot"].wait()
     cot_right = [cot_copy(at, u, cot_own_send.at[0], at + 2) for u in range(PARTS)]
@@ -128,74 +141,85 @@
     for copy in cot_across:
         copy.start()
 
-    def y_copy(t, j, h):
+    def slot_of(p, src, i):
+        j, offset, width = pieces[i]
+        return msg.at[p, src, j, :, pl.ds(offset, width)]
+
+    def message(p, src, i, send_sem, target):
         return pltpu.make_async_remote_copy(
-            src_ref=msg.at[c, y, j, h], dst_ref=msg.at[c, y, j, h],
-            send_sem=y_send.at[t - 1, j, h], recv_sem=msg_recv.at[c, y, j, h],
-            device_id={"replica": lax.rem(me + 2 * t, R)}, device_id_type=MESH)
-
-    def to_sib(src, j, h):
-        return pltpu.make_async_remote_copy(
-            src_ref=msg.at[c, src, j, h], dst_ref=msg.at[c, src, j, h],
-            send_sem=fwd_send.at[src, j, h], recv_sem=msg_recv.at[c, src, j, h],
-            device_id={"replica": sib}, device_id_type=MESH)
-
-    def arrival(p, src, j, h):
-        return pltpu.make_async_remote_copy(
-            src_ref=msg.at[p, src, j, h], dst_ref=msg.at[p, src, j, h],
-            send_sem=fwd_send.at[src, j, h], recv_sem=msg_recv.at[p, src, j, h],
-            device_id={"replica": sib}, device_id_type=MESH)
+            src_ref=slot_of(p, src, i), dst_ref=slot_of(p, src, i),
+            send_sem=send_sem, recv_sem=msg_recv.at[p, src, i],
+            device_id={"replica": target}, device_id_type=MESH)
+
+    def y_copy(t, i):
+        return message(c, y, i, y_send.at[t - 1, i], lax.rem(me + 2 * t, R))
+
+    def cross_copy(t):
+        return message(c, y, last, cross_send.at[t - 1], lax.rem(sib + 2 * t, R))
+
+    def to_sib(src, i):
+        return message(c, src, i, fwd_send.at[src, i], sib)
+
+    def arrival(p, src, i):
+        return message(p, src, i, fwd_send.at[src, i], sib)
 
     c1 = outer_rate * (1.0 + momentum_keep)
     c2 = outer_rate * momentum_keep * momentum_keep
     share = c1 / R
-    for j in range(C):
-        loads[("keep", j)].wait()
-        if j == 0:
+    for i, (j, offset, width) in enumerate(pieces):
+        if offset == 0:
+            loads[("keep", j)].wait()
+        if i == 0:
             loads["anchor"].wait()
             loads["vel"].wait()
         mine = y == j
         of_anchor = jnp.where(mine, 0.0, 2.0)
         of_rows = jnp.where(mine, share, -1.0)
         of_vel = jnp.where(mine, -c2, 0.0)
-        for h in range(H):
-            sib_copy(j, h).wait_recv()
-            cols = columns(2 * j + c, h)
-            both = rows[:, cols].astype(jnp.float32) + sib_rows[j, h].astype(jnp.float32)
-            value = of_anchor * anchor[:, cols] + of_rows * both
-            value = value + of_vel * vel[:, h * piece:(h + 1) * piece]
-            msg[c, y, j, h] = value.astype(jnp.bfloat16)
-            for t in range(1, C):
-                y_copy(t, j, h).start()
-            to_sib(y, j, h).start()
-
-    def finish(p, j, h):
-        cols = columns(2 * j + p, h)
-        others = msg[p, (j + 1) % C, j, h].astype(jnp.float32)
+        sib_copy(i).wait_recv()
+        cols = columns(2 * j + c, offset, width)
+        part = slice(offset, offset + width)
+        both = rows[:, cols].astype(jnp.float32) + sib_rows[j, :, part].astype(jnp.float32)
+        value = of_anchor * anchor[:, cols] + of_rows * both
+        value = value + of_vel * vel[:, part]
+        msg[c, y, j, :, part] = value.astype(jnp.bfloat16)
+        for t in range(1, C):
+            y_copy(t, i).start()
+            if i == last:
+                cross_copy(t).start()
+        to_sib(y, i).start()
+
+    def finish(p, i):
+        j, offset, width = pieces[i]
+        cols = columns(2 * j + p, offset, width)
+        part = slice(offset, offset + width)
+        others = msg[p, (j + 1) % C, j, :, part].astype(jnp.float32)
         for t in range(2, C):
-            others = others + msg[p, (j + t) % C, j, h].astype(jnp.float32)
-        own = msg[p, j, j, h].astype(jnp.float32)
+            others = others + msg[p, (j + t) % C, j, :, part].astype(jnp.float32)
+        own = msg[p, j, j, :, part].astype(jnp.float32)
         new_anchor = (1.0 - 2.0 * share) * anchor[:, cols] + own - share * others
         na_o[:, cols] = new_anchor
         mg_o[0, :, cols] = (
             blend_keep * rows[:, cols].astype(jnp.float32) + (1.0 - blend_keep) * new_anchor
         ).astype(jnp.bfloat16)
 
-    def finish_velocity(j, h):
+    def finish_velocity(i):
+        j, offset, width = pieces[i]
+
         @pl.when(y == j)
         def _():
-            cols = columns(2 * j + c, h)
-            part = slice(h * piece, (h + 1) * piece)
+            cols = columns(2 * j + c, offset, width)
+            part = slice(offset, offset + width)
             total = 2.0 * anchor[:, cols] - (
-                rows[:, cols].astype(jnp.float32) + sib_rows[j, h].astype(jnp.float32))
+                rows[:, cols].astype(jnp.float32) + sib_rows[j, :, part].astype(jnp.float32))
             for t in range(1, C):
-                total = total + msg[c, (j + t) % C, j, h].astype(jnp.float32)
+                total = total + msg[c, (j + t) % C, j, :, part].astype(jnp.float32)
             nv_o[:, part] = momentum_keep * vel[:, part] + total / R
 
-    def finish_sib(j, h):
+    def finish_sib(i):
         for src in range(C):
-            arrival(1 - c, src, j, h).wait_recv()
-        finish(1 - c, j, h)
+            arrival(1 - c, src, i).wait_recv()
+        finish(1 - c, i)
 
     def cot_step(t, u):
         @pl.when(pos >= t)
@@ -220,49 +244,53 @@
 
             cot_copy(k, u, cot_x_send.at[k // 2], partner).start()
 
-    pieces = [(j, h) for j in range(C) for h in range(H)]
+    def inner_step():
+        for k in range(length):
+            for u in range(PARTS):
+                cot_copy(2 * k + 1 - at % 2, u, cot_x_send.at[0], partner).wait_recv()
+        for name in ("feat", "w", "m", "s"):
+            loads[name].wait()
+        tile = min(256, w.shape[1])
+        for n in range(w.shape[1] // tile):
+            part = slice(n * tile, (n + 1) * tile)
+            gradient = jnp.dot(feat[...], cot[:, part], preferred_element_type=jnp.float32)
+            new_first = decay_first * m[:, part] + (1.0 - decay_first) * gradient
+            new_second = decay_second * s[:, part] + (1.0 - decay_second) * gradient * gradient
+            stepped = new_first / first_fix / (jnp.sqrt(new_second / second_fix) + epsilon)
+            weight = w[:, part]
+            nw_o[0, :, part] = weight - inner_rate * (stepped + weight_decay * weight)
+            nm_o[0, :, part] = new_first
+            ns_o[0, :, part] = new_second
+
     todo = [(t, u) for t in range(1, length) for u in range(PARTS)]
-    before = None
-    for i, (j, h) in enumerate(pieces):
-        while todo and 3 * (todo[0][0] - 1) + todo[0][1] <= i + 2:
+    for i in range(len(pieces)):
+        while i < last and todo and 3 * (todo[0][0] - 1) + todo[0][1] <= i + 1:
             cot_step(*todo.pop(0))
+        if i == last:
+            for step in todo:
+                cot_step(*step)
+            inner_step()
+            finish_sib(last - 1)
         for t in range(1, C):
             src = lax.rem(y + t, C)
-            arrival(c, src, j, h).wait_recv()
-            to_sib(src, j, h).start()
-        finish(c, j, h)
-        finish_velocity(j, h)
-        if before is not None:
-            finish_sib(*before)
-        before = (j, h)
-    for step in todo:
-        cot_step(*step)
-
-    for k in range(length):
-        for u in range(PARTS):
-            cot_copy(2 * k + 1 - at % 2, u, cot_x_send.at[0], partner).wait_recv()
-    for name in ("feat", "w", "m", "s"):
-        loads[name].wait()
-    tile = min(256, w.shape[1])
-    for n in range(w.shape[1] // tile):
-        part = slice(n * tile, (n + 1) * tile)
-        gradient = jnp.dot(feat[...], cot[:, part], preferred_element_type=jnp.float32)
-        new_first = decay_first * m[:, part] + (1.0 - decay_first) * gradient
-        new_second = decay_second * s[:, part] + (1.0 - decay_second) * gradient * gradient
-        stepped = new_first / first_fix / (jnp.sqrt(new_second / second_fix) + epsilon)
-        weight = w[:, part]
-        nw_o[0, :, part] = weight - inner_rate * (stepped + weight_decay * weight)
-        nm_o[0, :, part] = new_first
-        ns_o[0, :, part] = new_second
-
-    finish_sib(*before)
-
-    for j, h in pieces:
-        sib_copy(j, h).wait_send()
+            arrival(c, src, i).wait_recv()
+            if i < last:
+                to_sib(src, i).start()
+        finish(c, i)
+        finish_velocity(i)
+        if 0 < i < last:
+            finish_sib(i - 1)
+    finish_sib(last)
+
+    for i in range(len(pieces)):
+        sib_copy(i).wait_send()
         for t in range(1, C):
-            y_copy(t, j, h).wait_send()
-        for src in range(C):
-            to_sib(src, j, h).wait_send()
+            y_copy(t, i).wait_send()
+            if i == last:
+                cross_copy(t).wait_send()
+            else:
+                to_sib(lax.rem(y + t, C), i).wait_send()
+        to_sib(y, i).wait_send()
     for copy in cot_across:
         copy.wait_send()
 
@@ -329,9 +357,10 @@
 
 def local(R, S, anchor, replica_rows, outer_velocity, features, cotangent,
           inner_weight, first_moment, second_moment):
-    C, H = R // 2, SPLIT
+    C = R // 2
     depth_rows = anchor.shape[0]
     W = outer_velocity.shape[1]
+    N = len(pieces_of(C, W))
     f32, bf16 = jnp.float32, jnp.bfloat16
     args = (anchor, replica_rows, outer_velocity, features, cotangent,
             inner_weight, first_moment, second_moment)
@@ -353,14 +382,15 @@
             pltpu.VMEM(inner_weight.shape[1:], f32),
             pltpu.VMEM(inner_weight.shape[1:], f32),
             pltpu.VMEM(inner_weight.shape[1:], f32),
-            pltpu.VMEM((C, H, depth_rows, W // H), bf16),
-            pltpu.VMEM((2, C, C, H, depth_rows, W // H), bf16),
+            pltpu.VMEM((C, depth_rows, W), bf16),
+            pltpu.VMEM((2, C, C, depth_rows, W), bf16),
             dma((7 + 2 * C,)),
-            dma((C, H)),
-            dma((C, H)),
-            dma((C - 1, C, H)),
-            dma((C, C, H)),
-            dma((2, C, C, H)),
+            dma((N,)),
+            dma((N,)),
+            dma((C - 1, N)),
+            dma((C - 1,)),
+            dma((C, N)),
+            dma((2, C, N)),
             dma((3, PARTS)),
             dma((2, max(length - 1, 1), PARTS)),
             dma((length, PARTS)),

time: 21.4 us -> 21.8 us (1.019)
  Pallas kernels: 20.6 us -> 21 us
    pallas_call x1, Pallas kernels: 18.8 us -> 19.1 us  [local(): pl.pallas_call(functools.partial(kernel, R, S), out_shape=tuple((pltpu.VM...]
where the time goes in v3:
time: 21.8 us; the launch traced here: 21.6 us
  Pallas kernels  21 us (96%)
  between operations  0.64 us (3%)
    pallas_call x1, Pallas kernels, local(): pl.pallas_call(functools.partial(kernel, R, S), out_shape=tuple((pltpu.VM...  19.1 us
    pallas_call x1, Pallas kernels, store(): pl.pallas_call(store_kernel, out_shape=tuple((jax.ShapeDtypeStruct(a.shap...  1.87 us

profile of v3, /device:TPU:0, one launch (start us, length us, event | category | flops | bytes accessed | tf_op | source)
XLA Modules:
  0.0 21.6 jit_solution(7545579668666312045)
XLA Ops:
  0.6 19.1 %shard_map.127 = (f32[48,8192]{1,0:T(8,128)S(1)}, bf16[1,48,8192]{2,1,0:T(8,128)(2,1)S(1)}, f32[48,2048]{1,0:T(8,128)S(1)}, f32[1,48,1024]{2,1,0:T(8,128)S(1)}, ...) custom-call(f32[48,8192]{1,0:T(8,128)} %anchor_h.1, bf16[1,48,8192]{2,1,0:T(8,128)(2,1)} %rows_h.1, ...), custom_call_target="tpu_custom_call" | custom-call | tf_op jit(solution)/shard_map/pallas_call | solution.py:371
  19.8 1.9 %shard_map.128 = (f32[48,8192]{1,0:T(8,128)}, bf16[1,48,8192]{2,1,0:T(8,128)(2,1)}, f32[48,2048]{1,0:T(8,128)}, f32[1,48,1024]{2,1,0:T(8,128)}, f32[1,48,1024]{2,1,0:T(8,128)}, /*index=5*/f32[1,48,1024]{2,1,0:T(8,128)}) custom-call(f32[48,8192]{1,0:T(8,128)S(1)} %get-tuple-element.12.refs_0_, bf16[1,48,8192]{2,1,0:T(8,128)(2,1)S(1)} %get-tuple-element.13.refs_1_, ...), custom_call_target="tpu_custom_call" | custom-call | tf_op jit(solution)/shard_map/pallas_call | solution.py:348

commit v4 on v2

--- a/solution.py
+++ b/solution.py
@@ -20,7 +20,7 @@
 
 MESH = pl.DeviceIdType.MESH
 SPLIT = 4
-PARTS = 2
+PARTS = 4
 
 
 def kernel(R, S, anchor_h, rows_h, vel_h, feat_h, cot_h, w_h, m_h, s_h,
@@ -38,7 +38,7 @@
     W = vel.shape[1]
     piece = W // H
     depth = cot_h.shape[1]
-    part_depth = depth // PARTS
+    part_width = cot_h.shape[2] // PARTS
 
     def columns(q, h):
         return pl.ds(pl.multiple_of(q * W + h * piece, 128), piece)
@@ -49,8 +49,8 @@
     def tokens(k):
         return pl.ds(pl.multiple_of(k * depth, depth), depth)
 
-    def half_tokens(k, u):
-        return pl.ds(pl.multiple_of(k * depth + u * part_depth, part_depth), part_depth)
+    def block_part(k, u):
+        return cot.at[tokens(k), pl.ds(u * part_width, part_width)]
 
     barrier = pltpu.get_barrier_semaphore()
     pl.semaphore_signal(barrier, inc=1, device_id={"replica": sib}, device_id_type=MESH)
@@ -101,7 +101,7 @@
 
     def cot_copy(k, u, send_sem, target):
         return pltpu.make_async_remote_copy(
-            src_ref=cot.at[half_tokens(k, u)], dst_ref=cot.at[half_tokens(k, u)],
+            src_ref=block_part(k, u), dst_ref=block_part(k, u),
             send_sem=send_sem.at[u], recv_sem=cot_recv.at[k, u],
             device_id={"shard": target}, device_id_type=MESH)
 
@@ -224,7 +224,7 @@
     todo = [(t, u) for t in range(1, length) for u in range(PARTS)]
     before = None
     for i, (j, h) in enumerate(pieces):
-        while todo and 3 * (todo[0][0] - 1) + todo[0][1] <= i + 2:
+        while todo and 3 * (todo[0][0] - 1) + todo[0][1] // 2 <= i + 2:
             cot_step(*todo.pop(0))
         for t in range(1, C):
             src = lax.rem(y + t, C)

time: 21.4 us -> 21.3 us (level)
  no operation moved by 1% of the time
where the time goes in v4:
time: 21.3 us; the launch traced here: 21.2 us
  Pallas kernels  20.5 us (96%)
  between operations  0.64 us (3%)
    pallas_call x1, Pallas kernels, local(): pl.pallas_call(functools.partial(kernel, R, S), out_shape=tuple((pltpu.VM...  18.7 us
    pallas_call x1, Pallas kernels, store(): pl.pallas_call(store_kernel, out_shape=tuple((jax.ShapeDtypeStruct(a.shap...  1.87 us

profile of v4, /device:TPU:0, one launch (start us, length us, event | category | flops | bytes accessed | tf_op | source)
XLA Modules:
  0.0 21.2 jit_solution(2741369296660889941)
XLA Ops:
  0.6 18.7 %shard_map.127 = (f32[48,8192]{1,0:T(8,128)S(1)}, bf16[1,48,8192]{2,1,0:T(8,128)(2,1)S(1)}, f32[48,2048]{1,0:T(8,128)S(1)}, f32[1,48,1024]{2,1,0:T(8,128)S(1)}, ...) custom-call(f32[48,8192]{1,0:T(8,128)} %anchor_h.1, bf16[1,48,8192]{2,1,0:T(8,128)(2,1)} %rows_h.1, ...), custom_call_target="tpu_custom_call" | custom-call | tf_op jit(solution)/shard_map/pallas_call | solution.py:342
  19.3 1.9 %shard_map.128 = (f32[48,8192]{1,0:T(8,128)}, bf16[1,48,8192]{2,1,0:T(8,128)(2,1)}, f32[48,2048]{1,0:T(8,128)}, f32[1,48,1024]{2,1,0:T(8,128)}, f32[1,48,1024]{2,1,0:T(8,128)}, /*index=5*/f32[1,48,1024]{2,1,0:T(8,128)}) custom-call(f32[48,8192]{1,0:T(8,128)S(1)} %get-tuple-element.12.refs_0_, bf16[1,48,8192]{2,1,0:T(8,128)(2,1)S(1)} %get-tuple-element.13.refs_1_, ...), custom_call_target="tpu_custom_call" | custom-call | tf_op jit(solution)/shard_map/pallas_call | solution.py:320
